TPU v7x, 128 devices: a whole 4x4x4 slice. The times are simulated.
128 devices in a mesh: sp: 8 (over z, core), tp: 16 (over x, y).
Axes of the slice: x: 4, y: 4, z: 4, core: 2. Of those that a mesh axis runs over, the one named last changes fastest.
Arguments:
- tokens: bfloat16 [16384, 2048], P(('sp', 'tp')), may hold values from -3 to 3
- queries: bfloat16 [16384, 2048], P(('sp', 'tp')), may hold values from -140 to 140
- keys: bfloat16 [16384, 1024], P(('sp', 'tp')), may hold values from -6 to 6
- values: bfloat16 [16384, 1024], P(('sp', 'tp')), may hold values from -6 to 6
- out_weight: bfloat16 [2048, 2048], P('sp', 'tp'), may hold values from -0.25 to 0.25
- norm_gain: bfloat16 [2048], replicated, may hold values from 0.099609375 to 1.8984375
- gate_weight: bfloat16 [2048, 7168], P('sp', 'tp'), may hold values from -0.125 to 0.125
- up_weight: bfloat16 [2048, 7168], P('sp', 'tp'), may hold values from -0.125 to 0.125
- down_weight: bfloat16 [7168, 2048], P('tp', 'sp'), may hold values from -0.125 to 0.125
Outputs:
- attended: bfloat16 [16384, 2048], P(('sp', 'tp'))
- layer_out: bfloat16 [16384, 2048], P(('sp', 'tp'))
All inputs are finite; a program needn't handle non-finite values.
Results may differ from a plain program's by a relative error of at most 0.023.
Values may be sent and summed in bfloat16 or wider, within the bound.
No kernel may reach another device: no remote copies, remote signals or barrier semaphores. Data moves between devices by JAX's collectives and lax.ppermute only.
A program may use at most 128 MiB of HBM per device.

v0:
```python
import jax
import jax.numpy as jnp
from jax import lax
from jax.sharding import PartitionSpec as P

HEAD_DIM = 128
norm_eps = 1e-05


def side_by_side(arrays, axis, dim, along):
    both = jnp.concatenate(arrays, axis=along)
    result, at, done = (lax.all_gather(both, axis, axis=dim, tiled=True), 0, [])
    for a in arrays:
        done.append(lax.slice_in_dim(result, at, at + a.shape[along], axis=along))
        at += a.shape[along]
    return tuple(done)


def sent_to_all(array, axis):
    copies = jnp.broadcast_to(array, (lax.axis_size(axis), *array.shape))
    return lax.all_to_all(copies, axis, split_axis=0, concat_axis=0, tiled=True)


def joined_along(blocks, dim):
    dims = list(blocks.shape[1:])
    dims[dim] *= blocks.shape[0]
    return jnp.moveaxis(blocks, 0, dim).reshape(dims)


def gather_directly(array, axis, dim):
    blocks = sent_to_all(array, axis)
    return joined_along(blocks, dim)


def attend(q_block, query_pos, k_block, v_block, key_pos, kv_local):
    row_count = q_block.shape[0]
    key_count = k_block.shape[0]
    q_four = q_block.reshape(row_count, kv_local, -1, HEAD_DIM)
    k_three = k_block.reshape(key_count, kv_local, HEAD_DIM)
    v_three = v_block.reshape(key_count, kv_local, HEAD_DIM)
    scores = jnp.einsum(
        "qhgd,khd->hgqk", q_four, k_three, preferred_element_type=jnp.float32
    ) * HEAD_DIM ** (-0.5)
    causal = key_pos[None, :] <= query_pos[:, None]
    scores = jnp.where(causal[None, None, :, :], scores, -1e30)
    row_peak = jnp.max(scores, axis=-1, keepdims=True)
    exp_terms = jnp.exp(scores - row_peak)
    probs = (exp_terms / jnp.sum(exp_terms, axis=-1, keepdims=True)).astype(jnp.bfloat16)
    mixed_out = jnp.einsum("hgqk,khd->qhgd", probs, v_three, preferred_element_type=jnp.float32)
    return mixed_out.astype(jnp.bfloat16).reshape(row_count, -1)


def add_rows(all_rows, weight_piece):
    return jnp.dot(all_rows, weight_piece, preferred_element_type=jnp.float32)


def shards(
    tokens, queries, keys, values, out_weight, norm_gain, gate_weight, up_weight, down_weight
):
    shard_rows = tokens.shape[0]
    sp_count = lax.axis_size("sp")
    tp_count = lax.axis_size("tp")
    segment_len = shard_rows * tp_count
    seq_len = segment_len * sp_count
    local_q = lax.all_to_all(queries, "sp", split_axis=1, concat_axis=0, tiled=True)
    part_keys, part_values = (
        lax.all_to_all(keys, "sp", split_axis=1, concat_axis=0, tiled=True),
        lax.all_to_all(values, "sp", split_axis=1, concat_axis=0, tiled=True),
    )
    width_kv = part_keys.shape[1]
    grid_keys, grid_values = side_by_side(
        (
            part_keys.reshape(sp_count, shard_rows, width_kv),
            part_values.reshape(sp_count, shard_rows, width_kv),
        ),
        "tp",
        1,
        0,
    )
    all_keys = grid_keys.reshape(seq_len, width_kv)
    all_values = grid_values.reshape(seq_len, width_kv)
    kv_local = all_keys.shape[1] // HEAD_DIM
    query_index = jnp.arange(sp_count * shard_rows, dtype=jnp.int32)
    query_pos = (
        query_index // shard_rows * segment_len
        + lax.axis_index("tp") * shard_rows
        + query_index % shard_rows
    )
    key_pos = jnp.arange(seq_len, dtype=jnp.int32)
    pieces_out = []
    for segment in range(sp_count):
        first_row = segment * shard_rows
        key_reach = (segment + 1) * segment_len
        pieces_out.append(
            attend(
                local_q[first_row : first_row + shard_rows],
                query_pos[first_row : first_row + shard_rows],
                all_keys[:key_reach],
                all_values[:key_reach],
                key_pos[:key_reach],
                kv_local,
            )
        )
    attn = jnp.concatenate(pieces_out, axis=0)
    wo_full = lax.all_gather(out_weight, "tp", axis=1, tiled=True)
    block_rows = attn
    attn_part = lax.psum_scatter(
        jnp.dot(block_rows, wo_full, preferred_element_type=jnp.float32).astype(jnp.bfloat16),
        "sp",
        scatter_dimension=0,
        tiled=True,
    ).astype(jnp.float32)
    attended = (tokens.astype(jnp.float32) + attn_part).astype(jnp.bfloat16)
    attended_wide = attended.astype(jnp.float32)
    inverse_rms = lax.rsqrt(
        jnp.mean(attended_wide * attended_wide, axis=1, keepdims=True) + norm_eps
    )
    normed = (attended_wide * inverse_rms * norm_gain.astype(jnp.float32)).astype(jnp.bfloat16)
    all_rows = lax.all_gather(normed, "tp", axis=0, tiled=True)

    def add_single(weight_piece):
        return add_rows(all_rows, weight_piece)

    gate_sum = add_single(gather_directly(gate_weight, "sp", 0))
    up_sum = add_single(lax.all_gather(up_weight, "sp", axis=0, tiled=True))
    hidden = (jax.nn.silu(gate_sum) * up_sum).astype(jnp.bfloat16)
    down_full = lax.all_gather(down_weight, "sp", axis=1, tiled=True)
    block_rows = hidden
    ffn_part = lax.psum_scatter(
        jnp.dot(block_rows, down_full, preferred_element_type=jnp.float32).astype(jnp.bfloat16),
        "tp",
        scatter_dimension=0,
        tiled=True,
    ).astype(jnp.float32)
    layer_out = (attended_wide + ffn_part).astype(jnp.bfloat16)
    return (attended, layer_out)


def solution(mesh):
    return jax.shard_map(
        shards,
        mesh=mesh,
        in_specs=(
            P(("sp", "tp"), None),
            P(("sp", "tp"), None),
            P(("sp", "tp"), None),
            P(("sp", "tp"), None),
            P("sp", "tp"),
            P(),
            P("sp", "tp"),
            P("sp", "tp"),
            P("tp", "sp"),
        ),
        out_specs=(P(("sp", "tp"), None), P(("sp", "tp"), None)),
        check_vma=False,
    )
```

profile of v0, /device:TPU:0, one launch (start us, length us, event | category | flops | bytes accessed | tf_op | source)
XLA Modules:
  0.0 448.6 jit_solution(11308070882767555244)
XLA Ops:
  7.2 1.2 copy.89
  9.2 5.4 %all-to-all-start.1 = ((bf16[128,8,128]{2,0,1:T(8,128)(2,1)}), bf16[128,8,128]{2,0,1:T(8,128)(2,1)S(1)}, u32[]{:S(2)}, u32[]{:S(2)}) async-start(bf16[128,8,128]{2,0,1:T(8,128)(2,1)} %copy.90), calls=%async_computation.1 | async-start | bytes 524288 | tf_op jit(solution)/shard_map/all_to_all | solution.py:68
  16.0 6.1 %all-to-all-done.1 = bf16[128,8,128]{2,0,1:T(8,128)(2,1)S(1)} async-done(((bf16[128,8,128]{2,0,1:T(8,128)(2,1)}), bf16[128,8,128]{2,0,1:T(8,128)(2,1)S(1)}, u32[]{:S(2)}, u32[]{:S(2)}) %all-to-all-start.1) | async-done | bytes 262176 | tf_op jit(solution)/shard_map/all_to_all | solution.py:68
  22.1 9.9 %all_to_all.53 = bf16[128,8,128]{2,0,1:T(8,128)(2,1)S(1)} all-to-all(bf16[128,8,128]{2,0,1:T(8,128)(2,1)S(1)} %copy.88), channel_id=1, replica_groups=mesh['sp'=8,'tp'=16] {'sp'}, dimensions={1} | all-to-all | bytes 524288 | tf_op jit(solution)/shard_map/all_to_all | solution.py:67
  33.9 3.5 all-to-all-start.2
  38.3 2.4 iota_compare_fusion
  40.7 1.8 broadcast_compare_fusion.5
  42.6 3.4 broadcast_compare_fusion.4
  46.0 4.4 broadcast_compare_fusion.3
  50.4 5.5 %broadcast_compare_fusion.2 = pred[128,10240]{0,1:T(8,128)(4,1)} fusion(s32[128]{0:T(128)S(1)} %get-tuple-element.29, s32[10240]{0:T(1024)S(1)} %iota_add_fusion.2), kind=kLoop, calls=%fused_computation.62 | loop fusion | flops 1310720 | bytes 1352192 | tf_op jit(solution)/shard_map/le | solution.py:44
  55.9 6.4 %broadcast_compare_fusion.1 = pred[128,12288]{0,1:T(8,128)(4,1)} fusion(s32[128]{0:T(128)S(1)} %get-tuple-element.28, s32[12288]{0:T(1024)S(1)} %iota_add_fusion.1), kind=kLoop, calls=%fused_computation.59 | loop fusion | flops 1572864 | bytes 1622528 | tf_op jit(solution)/shard_map/le | solution.py:44
  62.3 6.7 %broadcast_compare_fusion = pred[128,14336]{0,1:T(8,128)(4,1)S(1)} fusion(s32[128]{0:T(128)S(1)} %get-tuple-element.27, s32[14336]{0:T(1024)S(1)} %iota_add_fusion), kind=kLoop, calls=%fused_computation.56 | loop fusion | flops 1835008 | bytes 1892864 | tf_op jit(solution)/shard_map/le | solution.py:44
  70.1 33.2 %all-gather.6.cloned.1.call-done = bf16[16,2048,128]{2,1,0:T(8,128)(2,1)} async-done(((bf16[16,128,128]{2,1,0:T(8,128)(2,1)}), bf16[16,2048,128]{2,1,0:T(8,128)(2,1)}) %all-gather.6.cloned.1.call-update) | async-done | bytes 8388624 | tf_op jit(solution)/shard_map/all_gather | solution.py:12
  103.2 1.6 fusion.83
  105.1 1.7 convolution_convert_fusion.2
  106.9 1.8 copy-done
  112.3 1.3 fusion.85
  114.5 1.3 fusion.41
  117.1 1.8 fusion.86
  120.0 1.7 fusion.44
  123.1 2.2 fusion.87
  125.3 1.4 fusion.13
  126.7 2.1 fusion.47
  130.2 2.7 fusion.88
  132.9 1.7 fusion.10
  134.7 2.5 fusion.50
  137.7 6.8 %fusion.89 = (f32[2,128]{1,0:T(2,128)S(1)}, f32[1,2,128,14336]{2,3,1,0:T(8,128)}) fusion(bf16[14336,128,1]{1,0,2:T(8,128)(2,1)S(1)} %bitcast.229, bf16[128,2,128]{0,2,1:T(8,128)(2,1)S(1)} %bitcast.247, pred[128,14336]{0,1:T(8,128)(4,1)S(1)} %broadcast_compare_fusion), kind=kOutput, calls=%fused_computation.138 | convolution fusion | flops 950533888 | bytes 20251648 | tf_op jit(solution)/shard_map/qhgd,khd->hgqk/dot_general | solution.py:41
  144.6 7.4 %fusion.8 = f32[2,128]{1,0:T(2,128)S(1)} fusion(f32[1,2,128,14336]{2,3,1,0:T(8,128)} %get-tuple-element.47, f32[2,128]{1,0:T(2,128)S(1)} %get-tuple-element.46), kind=kLoop, calls=%fused_computation.16 | loop fusion | flops 7339776 | bytes 14682112 | tf_op jit(solution)/shard_map/reduce_sum | solution.py:48
  152.0 6.9 %fusion.53 = bf16[128,2,128]{2,0,1:T(8,128)(2,1)S(1)} fusion(bf16[14336,128,1]{1,0,2:T(8,128)(2,1)S(1)} %bitcast.228, f32[2,128]{1,0:T(2,128)S(1)} %fusion.8, f32[1,2,128,14336]{2,3,1,0:T(8,128)} %get-tuple-element.47, f32[2,128]{1,0:T(2,128)S(1)} %get-tuple-element.46), kind=kOutput, calls=%fused_computation.79 | convolution fusion | flops 950566912 | bytes 18417664 | tf_op jit(solution)/shard_map/hgqk,khd->qhgd/dot_general | solution.py:49
  158.9 2.2 fusion.74
  161.2 5.2 %fusion.90 = (f32[2,128]{1,0:T(2,128)S(1)}, f32[1,2,128,16384]{2,3,1,0:T(8,128)S(1)}) fusion(bf16[16384,128,1]{1,0,2:T(8,128)(2,1)} %bitcast.227, bf16[128,2,128]{0,2,1:T(8,128)(2,1)S(1)} %bitcast.246, pred[128,16384]{0,1:T(8,128)(4,1)S(1)} %copy-done.2), kind=kOutput, calls=%fused_computation.139 | convolution fusion | flops 1086324480 | bytes 23135232 | tf_op jit(solution)/shard_map/qhgd,khd->hgqk/dot_general | solution.py:41
  166.4 4.4 fusion.6
  170.8 3.2 fusion.56
  174.1 4.5 %convolution_convert_fusion.1 = bf16[1024,2048]{1,0:T(8,128)(2,1)} fusion(bf16[1024,256]{0,1:T(8,128)(2,1)S(1)} %constant_dynamic-update-slice_fusion, bf16[256,2048]{1,0:T(8,128)(2,1)} %all-gather.8.cloned.1.call-done), kind=kOutput, calls=%fused_computation.53 | convolution fusion | flops 1075838976 | bytes 5767168 | tf_op jit(solution)/shard_map/dot_general | solution.py:108
  178.7 37.9 %reduce-scatter.3.cloned.1.call-done = bf16[128,2048]{1,0:T(8,128)(2,1)} async-done(((bf16[1024,2048]{1,0:T(8,128)(2,1)}), bf16[128,2048]{1,0:T(8,128)(2,1)}) %reduce-scatter.3.cloned.1.call-update) | async-done | bytes 524304 | tf_op jit(solution)/shard_map/reduce_scatter | solution.py:107
  216.6 1.3 fusion.59
  219.6 1.4 broadcast_in_dim.157
  221.0 3.6 all-to-all-start.3
  225.4 23.5 %all-to-all-done.3 = bf16[8,256,448]{1,2,0:T(8,128)(2,1)S(1)} async-done(((bf16[8,256,448]{1,2,0:T(8,128)(2,1)}), bf16[8,256,448]{1,2,0:T(8,128)(2,1)S(1)}, u32[]{:S(2)}, u32[]{:S(2)}) %all-to-all-start.3) | async-done | bytes 1835040 | tf_op jit(solution)/shard_map/all_to_all | solution.py:21
  248.9 1.5 copy.149
  250.3 38.4 %all-gather.10.cloned.1.call-done = bf16[2048,2048]{1,0:T(8,128)(2,1)} async-done(((bf16[128,2048]{1,0:T(8,128)(2,1)}), bf16[2048,2048]{1,0:T(8,128)(2,1)}) %all-gather.10.cloned.1.call-update) | async-done | bytes 8388624 | tf_op jit(solution)/shard_map/all_gather | solution.py:119
  288.7 9.7 %fusion.91 = f32[2048,448]{0,1:T(8,128)} fusion(bf16[2048,2048]{1,0:T(8,128)(2,1)} %all-gather.10.cloned.1.call-done, bf16[2048,448]{0,1:T(8,128)(2,1)} %bitcast.237), kind=kOutput, calls=%fused_computation.140 | convolution fusion | flops 3758096384 | bytes 13893632 | tf_op jit(solution)/shard_map/dot_general | solution.py:54
  298.4 17.6 %all-gather.12.cloned.1.call-done = bf16[2048,448]{0,1:T(8,128)(2,1)} async-done(((bf16[256,448]{0,1:T(8,128)(2,1)}), bf16[2048,448]{0,1:T(8,128)(2,1)}) %all-gather.12.cloned.1.call-update) | async-done | bytes 1835024 | tf_op jit(solution)/shard_map/all_gather | solution.py:125
  316.1 9.1 %multiply_convert_fusion = bf16[2048,448]{0,1:T(8,128)(2,1)S(1)} fusion(f32[2048,448]{0,1:T(8,128)} %fusion.91, bf16[2048,2048]{1,0:T(8,128)(2,1)} %all-gather.10.cloned.1.call-done, bf16[2048,448]{0,1:T(8,128)(2,1)} %all-gather.12.cloned.1.call-done), kind=kOutput, calls=%fused_computation.55 | convolution fusion | flops 3763601408 | bytes 15728640 | tf_op jit(solution)/shard_map/dot_general | solution.py:54
  325.2 19.3 %all-gather.14.cloned.1.call-done = bf16[448,2048]{1,0:T(8,128)(2,1)} async-done(((bf16[448,256]{1,0:T(8,128)(2,1)}), bf16[448,2048]{1,0:T(8,128)(2,1)}) %all-gather.14.cloned.1.call-update) | async-done | bytes 1835024 | tf_op jit(solution)/shard_map/all_gather | solution.py:127
  344.5 8.3 %convolution_convert_fusion = bf16[2048,2048]{1,0:T(8,128)(2,1)} fusion(bf16[2048,448]{0,1:T(8,128)(2,1)S(1)} %multiply_convert_fusion, bf16[448,2048]{1,0:T(8,128)(2,1)} %all-gather.14.cloned.1.call-done), kind=kOutput, calls=%fused_computation.34 | convolution fusion | flops 3762290688 | bytes 12058624 | tf_op jit(solution)/shard_map/dot_general | solution.py:130
  352.8 86.9 %reduce-scatter.5.cloned.1.call-done = bf16[128,2048]{1,0:T(8,128)(2,1)} async-done(((bf16[2048,2048]{1,0:T(8,128)(2,1)}), bf16[128,2048]{1,0:T(8,128)(2,1)}) %reduce-scatter.5.cloned.1.call-update) | async-done | bytes 524304 | tf_op jit(solution)/shard_map/reduce_scatter | solution.py:129
  439.6 2.0 fusion.62
  (88 shorter events, 19.0 us)
Async XLA Ops:
  7.2 25.7 %copy-start.7 = (bf16[128,2048]{1,0:T(8,128)(2,1)S(1)}, bf16[128,2048]{1,0:T(8,128)(2,1)}, u32[]{:S(2)}) copy-start(bf16[128,2048]{1,0:T(8,128)(2,1)} %param.10) | copy-start | bytes 1572868
  9.2 12.9 %all-to-all-start.1 = ((bf16[128,8,128]{2,0,1:T(8,128)(2,1)}), bf16[128,8,128]{2,0,1:T(8,128)(2,1)S(1)}, u32[]{:S(2)}, u32[]{:S(2)}) async-start(bf16[128,8,128]{2,0,1:T(8,128)(2,1)} %copy.90), calls=%async_computation.1 | async-start | bytes 524288 | tf_op jit(solution)/shard_map/all_to_all | solution.py:68
  14.6 88.6 %all-gather.6.cloned.1.call-start = ((), (), s32[]{:S(2)}) async-start(), calls=%async_computation.6 | async-start | bytes 8912896 | tf_op jit(solution)/shard_map/all_gather | solution.py:12
  33.9 35.4 %all-to-all-start.2 = ((bf16[128,8,256]{0,2,1:T(8,128)(2,1)}), bf16[128,8,256]{0,2,1:T(8,128)(2,1)S(1)}, u32[]{:S(2)}, u32[]{:S(2)}) async-start(bf16[128,8,256]{0,2,1:T(8,128)(2,1)} %bitcast.8), calls=%async_computation.2 | async-start | bytes 1048576 | tf_op jit(solution)/shard_map/all_to_all | solution.py:65
  37.4 136.7 %all-gather.8.cloned.1.call-start = ((), (), s32[]{:S(2)}) async-start(), calls=%async_computation.7 | async-start | bytes 1114112 | tf_op jit(solution)/shard_map/all_gather | solution.py:105
  38.2 178.5 %reduce-scatter.3.cloned.1.call-start = ((), (), s32[]{:S(2)}) async-start(), calls=%async_computation.8 | async-start | bytes 4718592 | tf_op jit(solution)/shard_map/reduce_scatter | solution.py:107
  105.1 3.5 copy-start
  106.8 1.9 copy-start.15
  111.2 1.1 copy-start.6
  111.2 1.1 copy-start.14
  115.9 1.2 copy-start.5
  115.9 1.2 copy-start.13
  121.7 1.3 copy-start.4
  121.8 1.3 copy-start.12
  128.8 1.4 copy-start.3
  128.8 1.4 copy-start.11
  158.9 2.3 copy-start.2
  158.9 2.3 copy-start.10
  174.1 4.6 %copy-start.16 = (bf16[2048]{0:T(1024)(128)(2,1)S(1)}, bf16[2048]{0:T(1024)(128)(2,1)}, u32[]{:S(2)}) copy-start(bf16[2048]{0:T(1024)(128)(2,1)} %param.14) | copy-start | bytes 12292
  174.1 42.6 %copy-start.8 = (bf16[128,2048]{1,0:T(8,128)(2,1)S(1)}, bf16[128,2048]{1,0:T(8,128)(2,1)}, u32[]{:S(2)}) copy-start(bf16[128,2048]{1,0:T(8,128)(2,1)} %param.9) | copy-start | bytes 1572868
  178.6 40.9 %copy-start.9 = (bf16[256,448]{0,1:T(8,128)(2,1)S(1)}, bf16[256,448]{0,1:T(8,128)(2,1)}, u32[]{:S(2)}) copy-start(bf16[256,448]{0,1:T(8,128)(2,1)} %param.15) | copy-start | bytes 688132
  178.6 110.1 %all-gather.10.cloned.1.call-start = ((), (), s32[]{:S(2)}) async-start(), calls=%async_computation.9 | async-start | bytes 8912896 | tf_op jit(solution)/shard_map/all_gather | solution.py:119
  217.9 221.7 %copy-start.1 = (bf16[128,2048]{1,0:T(8,128)(2,1)}, bf16[128,2048]{1,0:T(8,128)(2,1)S(1)}, u32[]{:S(2)}) copy-start(bf16[128,2048]{1,0:T(8,128)(2,1)S(1)} %get-tuple-element.3) | copy-start | bytes 1572868
  219.0 97.1 %all-gather.12.cloned.1.call-start = ((), (), s32[]{:S(2)}) async-start(), calls=%async_computation.10 | async-start | bytes 2064384 | tf_op jit(solution)/shard_map/all_gather | solution.py:125
  221.0 27.9 %all-to-all-start.3 = ((bf16[8,256,448]{1,2,0:T(8,128)(2,1)}), bf16[8,256,448]{1,2,0:T(8,128)(2,1)S(1)}, u32[]{:S(2)}, u32[]{:S(2)}) async-start(bf16[8,256,448]{1,2,0:T(8,128)(2,1)} %broadcast_in_dim.157), calls=%async_computation.4 | async-start | bytes 3670016 | tf_op jit(solution)/shard_map/all_to_all | solution.py:21
  224.6 119.9 %all-gather.14.cloned.1.call-start = ((), (), s32[]{:S(2)}) async-start(), calls=%async_computation.11 | async-start | bytes 2064384 | tf_op jit(solution)/shard_map/all_gather | solution.py:127
  225.2 214.5 %reduce-scatter.5.cloned.1.call-start = ((), (), s32[]{:S(2)}) async-start(), calls=%async_computation.12 | async-start | bytes 8912896 | tf_op jit(solution)/shard_map/reduce_scatter | solution.py:129
Sparse Core Ops, SparseCore 0:
  33.0 70.1 all-gather.5
  105.3 42.6 all-gather.7
  178.8 37.8 reduce-scatter.2
  219.2 69.4 all-gather.9
  290.2 25.7 all-gather.11
  317.6 26.8 all-gather.13
  352.9 86.7 reduce-scatter.4
where the time goes:
time: 454 us; the launch traced here: 449 us
  waiting for transfers between devices  265 us (58%)
  matrix products  74.5 us (16%)
  other arithmetic  53.9 us (12%)
  local copies, waits for them, and re-layouts  17.9 us (4%)
  between operations  14.8 us (3%)
  starting transfers between devices  13 us (3%)
  blocking collectives  9.9 us (2%)
    reduce_scatter x1, waiting for transfers between devices, shards(): lax.psum_scatter(jnp.dot(block_rows, down_full, preferred_element_type=jn...  86.9 us
    all_gather x1, waiting for transfers between devices, shards(): all_rows = lax.all_gather(normed, 'tp', axis=0, tiled=True)  38.4 us
    reduce_scatter x1, waiting for transfers between devices, shards(): lax.psum_scatter(jnp.dot(block_rows, wo_full, preferred_element_type=jnp....  37.9 us
    all_gather x1, waiting for transfers between devices, side_by_side(): result, at, done = (lax.all_gather(both, axis, axis=dim, tiled=True), 0, [])  33.2 us
    le x8, other arithmetic, attend(): causal = key_pos[None, :] <= query_pos[:, None]  31 us
    all_to_all x1, waiting for transfers between devices, sent_to_all(): return lax.all_to_all(copies, axis, split_axis=0, concat_axis=0, tiled=True)  23.5 us
    dot_general x8, matrix products, attend(): jnp.einsum('qhgd,khd->hgqk', q_four, k_three, preferred_element_type=jnp....  22.5 us
    dot_general x8, matrix products, attend(): jnp.einsum('hgqk,khd->qhgd', probs, v_three, preferred_element_type=jnp.f...  20.4 us
  transfers between devices with their start and end apart: 10, of which 8 were waited for; matrix products, arithmetic and copies ran while one was open for 27% of the time, Pallas kernels for 0%

commit v1 on v0

--- a/solution.py
+++ b/solution.py
@@ -1,3 +1,4 @@
+import functools
 import jax
 import jax.numpy as jnp
 from jax import lax
@@ -5,6 +6,21 @@
 
 HEAD_DIM = 128
 norm_eps = 1e-05
+
+
+def take_the_streams(block_here, array_dim):
+    return jnp.concatenate(
+        jax.lax.all_to_all(
+            jnp.stack(jax.lax.axis_size("tp") * [block_here]),
+            concat_axis=0,
+            split_axis=0,
+            axis_name="tp",
+        ),
+        array_dim,
+    )
+
+
+press_links = functools.partial(take_the_streams, array_dim=0)
 
 
 def side_by_side(arrays, axis, dim, along):
@@ -116,7 +132,7 @@
         jnp.mean(attended_wide * attended_wide, axis=1, keepdims=True) + norm_eps
     )
     normed = (attended_wide * inverse_rms * norm_gain.astype(jnp.float32)).astype(jnp.bfloat16)
-    all_rows = lax.all_gather(normed, "tp", axis=0, tiled=True)
+    all_rows = press_links(normed)
 
     def add_single(weight_piece):
         return add_rows(all_rows, weight_piece)

time: 454 us -> 520 us (1.15)
  waiting for transfers between devices: 265 us -> 319 us
  starting transfers between devices: 13 us -> 20.4 us
    all_to_all x0 -> x1, waiting for transfers between devices: none -> 124 us  [take_the_streams(): jax.lax.all_to_all(jnp.stack(jax.lax.axis_size('tp') * [block_here]), con...]
    all_gather x1 -> x0, waiting for transfers between devices: 38.4 us -> none  [shards(): all_rows = lax.all_gather(normed, 'tp', axis=0, tiled=True)]
    all_to_all x1, waiting for transfers between devices: 23.5 us -> 0.01 us  [sent_to_all(): return lax.all_to_all(copies, axis, split_axis=0, concat_axis=0, tiled=True)]
    reduce_scatter x1, waiting for transfers between devices: 86.9 us -> 108 us  [shards(): lax.psum_scatter(jnp.dot(block_rows, down_full, preferred_element_type=jn...]
    all_gather x1, waiting for transfers between devices: 19.3 us -> 0.02 us  [shards(): down_full = lax.all_gather(down_weight, 'sp', axis=1, tiled=True)]
    all_gather x1, waiting for transfers between devices: 17.6 us -> 0.01 us  [shards(): up_sum = add_single(lax.all_gather(up_weight, 'sp', axis=0, tiled=True))]
    reduce_scatter x1, waiting for transfers between devices: 37.9 us -> 46.7 us  [shards(): lax.psum_scatter(jnp.dot(block_rows, wo_full, preferred_element_type=jnp....]
    all_to_all x0 -> x1, starting transfers between devices: none -> 6.64 us  [take_the_streams(): jax.lax.all_to_all(jnp.stack(jax.lax.axis_size('tp') * [block_here]), con...]
  transfers between devices with their start and end apart: 10 -> 10, of which waited for: 8 -> 5; matrix products, arithmetic and copies ran while one was open for 27% -> 24% of each run, Pallas kernels for 0% -> 0%
where the time goes in v1:
time: 520 us; the launch traced here: 514 us
  waiting for transfers between devices  319 us (61%)
  matrix products  74.5 us (14%)
  other arithmetic  53.1 us (10%)
  local copies, waits for them, and re-layouts  22.2 us (4%)
  starting transfers between devices  20.4 us (4%)
  between operations  14.8 us (3%)
  blocking collectives  9.9 us (2%)
    all_to_all x1, waiting for transfers between devices, take_the_streams(): jax.lax.all_to_all(jnp.stack(jax.lax.axis_size('tp') * [block_here]), con...  124 us
    reduce_scatter x1, waiting for transfers between devices, shards(): lax.psum_scatter(jnp.dot(block_rows, down_full, preferred_element_type=jn...  108 us
    reduce_scatter x1, waiting for transfers between devices, shards(): lax.psum_scatter(jnp.dot(block_rows, wo_full, preferred_element_type=jnp....  46.7 us
    all_gather x1, waiting for transfers between devices, side_by_side(): result, at, done = (lax.all_gather(both, axis, axis=dim, tiled=True), 0, [])  33.1 us
    le x8, other arithmetic, attend(): causal = key_pos[None, :] <= query_pos[:, None]  31 us
    dot_general x8, matrix products, attend(): jnp.einsum('qhgd,khd->hgqk', q_four, k_three, preferred_element_type=jnp....  22.5 us
    dot_general x8, matrix products, attend(): jnp.einsum('hgqk,khd->qhgd', probs, v_three, preferred_element_type=jnp.f...  20.4 us
    dot_general x2, matrix products, add_rows(): return jnp.dot(all_rows, weight_piece, preferred_element_type=jnp.float32)  18.8 us
  transfers between devices with their start and end apart: 10, of which 5 were waited for; matrix products, arithmetic and copies ran while one was open for 24% of the time, Pallas kernels for 0%

profile of v1, /device:TPU:0, one launch (start us, length us, event | category | flops | bytes accessed | tf_op | source)
XLA Modules:
  0.0 514.2 jit_solution(17966744930001208946)
XLA Ops:
  7.2 1.2 copy.89
  9.2 5.4 %all-to-all-start.1 = ((bf16[128,8,128]{2,0,1:T(8,128)(2,1)}), bf16[128,8,128]{2,0,1:T(8,128)(2,1)S(1)}, u32[]{:S(2)}, u32[]{:S(2)}) async-start(bf16[128,8,128]{2,0,1:T(8,128)(2,1)} %copy.90), calls=%async_computation.1 | async-start | bytes 524288 | tf_op jit(solution)/shard_map/all_to_all | solution.py:84
  14.7 1.1 copy.87
  16.0 6.1 %all-to-all-done.1 = bf16[128,8,128]{2,0,1:T(8,128)(2,1)S(1)} async-done(((bf16[128,8,128]{2,0,1:T(8,128)(2,1)}), bf16[128,8,128]{2,0,1:T(8,128)(2,1)S(1)}, u32[]{:S(2)}, u32[]{:S(2)}) %all-to-all-start.1) | async-done | bytes 262176 | tf_op jit(solution)/shard_map/all_to_all | solution.py:84
  22.1 9.9 %all_to_all.58 = bf16[128,8,128]{2,0,1:T(8,128)(2,1)S(1)} all-to-all(bf16[128,8,128]{2,0,1:T(8,128)(2,1)S(1)} %copy.88), channel_id=1, replica_groups=mesh['sp'=8,'tp'=16] {'sp'}, dimensions={1} | all-to-all | bytes 524288 | tf_op jit(solution)/shard_map/all_to_all | solution.py:83
  33.9 3.5 all-to-all-start.2
  38.3 2.4 iota_compare_fusion
  40.7 1.8 broadcast_compare_fusion.5
  42.6 3.4 broadcast_compare_fusion.4
  46.0 4.4 broadcast_compare_fusion.3
  50.4 5.6 %broadcast_compare_fusion.2 = pred[128,10240]{0,1:T(8,128)(4,1)} fusion(s32[128]{0:T(128)S(1)} %get-tuple-element.29, s32[10240]{0:T(1024)S(1)} %iota_add_fusion.2), kind=kLoop, calls=%fused_computation.62 | loop fusion | flops 1310720 | bytes 1352192 | tf_op jit(solution)/shard_map/le | solution.py:60
  56.0 6.4 %broadcast_compare_fusion.1 = pred[128,12288]{0,1:T(8,128)(4,1)} fusion(s32[128]{0:T(128)S(1)} %get-tuple-element.28, s32[12288]{0:T(1024)S(1)} %iota_add_fusion.1), kind=kLoop, calls=%fused_computation.59 | loop fusion | flops 1572864 | bytes 1622528 | tf_op jit(solution)/shard_map/le | solution.py:60
  62.3 6.7 %broadcast_compare_fusion = pred[128,14336]{0,1:T(8,128)(4,1)S(1)} fusion(s32[128]{0:T(128)S(1)} %get-tuple-element.27, s32[14336]{0:T(1024)S(1)} %iota_add_fusion), kind=kLoop, calls=%fused_computation.56 | loop fusion | flops 1835008 | bytes 1892864 | tf_op jit(solution)/shard_map/le | solution.py:60
  70.1 33.1 %all-gather.5.cloned.1.call-done = bf16[16,2048,128]{2,1,0:T(8,128)(2,1)} async-done(((bf16[16,128,128]{2,1,0:T(8,128)(2,1)}), bf16[16,2048,128]{2,1,0:T(8,128)(2,1)}) %all-gather.5.cloned.1.call-update) | async-done | bytes 8388624 | tf_op jit(solution)/shard_map/all_gather | solution.py:28
  103.2 1.5 fusion.83
  105.1 1.7 convolution_convert_fusion.2
  106.9 1.8 copy-done
  112.3 1.3 fusion.85
  114.5 1.3 fusion.41
  117.1 1.8 fusion.86
  120.0 1.7 fusion.44
  123.1 2.2 fusion.87
  125.3 1.4 fusion.13
  126.7 2.1 fusion.47
  130.2 2.7 fusion.88
  132.9 1.7 fusion.10
  134.6 2.5 fusion.50
  137.7 6.9 %fusion.89 = (f32[2,128]{1,0:T(2,128)S(1)}, f32[1,2,128,14336]{2,3,1,0:T(8,128)}) fusion(bf16[14336,128,1]{1,0,2:T(8,128)(2,1)S(1)} %bitcast.230, bf16[128,2,128]{0,2,1:T(8,128)(2,1)S(1)} %bitcast.248, pred[128,14336]{0,1:T(8,128)(4,1)S(1)} %broadcast_compare_fusion), kind=kOutput, calls=%fused_computation.138 | convolution fusion | flops 950533888 | bytes 20251648 | tf_op jit(solution)/shard_map/qhgd,khd->hgqk/dot_general | solution.py:57
  144.6 7.4 %fusion.8 = f32[2,128]{1,0:T(2,128)S(1)} fusion(f32[1,2,128,14336]{2,3,1,0:T(8,128)} %get-tuple-element.47, f32[2,128]{1,0:T(2,128)S(1)} %get-tuple-element.46), kind=kLoop, calls=%fused_computation.16 | loop fusion | flops 7339776 | bytes 14682112 | tf_op jit(solution)/shard_map/reduce_sum | solution.py:64
  152.0 6.9 %fusion.53 = bf16[128,2,128]{2,0,1:T(8,128)(2,1)S(1)} fusion(bf16[14336,128,1]{1,0,2:T(8,128)(2,1)S(1)} %bitcast.229, f32[2,128]{1,0:T(2,128)S(1)} %fusion.8, f32[1,2,128,14336]{2,3,1,0:T(8,128)} %get-tuple-element.47, f32[2,128]{1,0:T(2,128)S(1)} %get-tuple-element.46), kind=kOutput, calls=%fused_computation.79 | convolution fusion | flops 950566912 | bytes 18417664 | tf_op jit(solution)/shard_map/hgqk,khd->qhgd/dot_general | solution.py:65
  158.9 2.2 fusion.74
  161.2 5.2 %fusion.90 = (f32[2,128]{1,0:T(2,128)S(1)}, f32[1,2,128,16384]{2,3,1,0:T(8,128)S(1)}) fusion(bf16[16384,128,1]{1,0,2:T(8,128)(2,1)} %bitcast.228, bf16[128,2,128]{0,2,1:T(8,128)(2,1)S(1)} %bitcast.247, pred[128,16384]{0,1:T(8,128)(4,1)S(1)} %copy-done.2), kind=kOutput, calls=%fused_computation.139 | convolution fusion | flops 1086324480 | bytes 23135232 | tf_op jit(solution)/shard_map/qhgd,khd->hgqk/dot_general | solution.py:57
  166.4 4.4 fusion.6
  170.8 3.2 fusion.56
  174.1 4.5 convolution_convert_fusion.1
  178.7 1.4 broadcast_in_dim.157
  180.1 4.4 all-to-all-start.4
  184.5 46.7 %reduce-scatter.3.cloned.1.call-done = bf16[128,2048]{1,0:T(8,128)(2,1)} async-done(((bf16[1024,2048]{1,0:T(8,128)(2,1)}), bf16[128,2048]{1,0:T(8,128)(2,1)}) %reduce-scatter.3.cloned.1.call-update) | async-done | bytes 524304 | tf_op jit(solution)/shard_map/reduce_scatter | solution.py:123
  231.2 1.3 fusion.59
  232.8 4.3 stack.2
  237.1 6.6 %all-to-all-start.3 = ((bf16[16,128,2048]{2,1,0:T(8,128)(2,1)}), bf16[16,128,2048]{2,1,0:T(8,128)(2,1)}, u32[]{:S(2)}, u32[]{:S(2)}) async-start(bf16[16,128,2048]{2,1,0:T(8,128)(2,1)} %stack.2), calls=%async_computation.4 | async-start | bytes 16777216 | tf_op jit(solution)/shard_map/all_to_all | solution.py:13
  245.1 1.5 copy.149
  246.6 123.7 %all-to-all-done.3 = bf16[16,128,2048]{2,1,0:T(8,128)(2,1)} async-done(((bf16[16,128,2048]{2,1,0:T(8,128)(2,1)}), bf16[16,128,2048]{2,1,0:T(8,128)(2,1)}, u32[]{:S(2)}, u32[]{:S(2)}) %all-to-all-start.3) | async-done | bytes 8388640 | tf_op jit(solution)/shard_map/all_to_all | solution.py:13
  370.3 9.7 %fusion.91 = f32[2048,448]{0,1:T(8,128)} fusion(bf16[2048,2048]{1,0:T(8,128)(2,1)} %bitcast.94, bf16[2048,448]{0,1:T(8,128)(2,1)} %bitcast.238), kind=kOutput, calls=%fused_computation.140 | convolution fusion | flops 3758096384 | bytes 13893632 | tf_op jit(solution)/shard_map/dot_general | solution.py:70
  380.0 9.1 %multiply_convert_fusion = bf16[2048,448]{0,1:T(8,128)(2,1)S(1)} fusion(f32[2048,448]{0,1:T(8,128)} %fusion.91, bf16[2048,2048]{1,0:T(8,128)(2,1)} %bitcast.94, bf16[2048,448]{0,1:T(8,128)(2,1)} %all-gather.9.cloned.1.call-done), kind=kOutput, calls=%fused_computation.55 | convolution fusion | flops 3763601408 | bytes 15728640 | tf_op jit(solution)/shard_map/dot_general | solution.py:70
  389.1 8.3 %convolution_convert_fusion = bf16[2048,2048]{1,0:T(8,128)(2,1)} fusion(bf16[2048,448]{0,1:T(8,128)(2,1)S(1)} %multiply_convert_fusion, bf16[448,2048]{1,0:T(8,128)(2,1)} %all-gather.11.cloned.1.call-done), kind=kOutput, calls=%fused_computation.34 | convolution fusion | flops 3762290688 | bytes 12058624 | tf_op jit(solution)/shard_map/dot_general | solution.py:146
  397.4 107.8 %reduce-scatter.5.cloned.1.call-done = bf16[128,2048]{1,0:T(8,128)(2,1)} async-done(((bf16[2048,2048]{1,0:T(8,128)(2,1)}), bf16[128,2048]{1,0:T(8,128)(2,1)}) %reduce-scatter.5.cloned.1.call-update) | async-done | bytes 524304 | tf_op jit(solution)/shard_map/reduce_scatter | solution.py:145
  505.2 2.0 fusion.62
  (88 shorter events, 17.0 us)
Async XLA Ops:
  7.2 25.7 %copy-start.7 = (bf16[128,2048]{1,0:T(8,128)(2,1)S(1)}, bf16[128,2048]{1,0:T(8,128)(2,1)}, u32[]{:S(2)}) copy-start(bf16[128,2048]{1,0:T(8,128)(2,1)} %param.10) | copy-start | bytes 1572868
  9.2 12.9 %all-to-all-start.1 = ((bf16[128,8,128]{2,0,1:T(8,128)(2,1)}), bf16[128,8,128]{2,0,1:T(8,128)(2,1)S(1)}, u32[]{:S(2)}, u32[]{:S(2)}) async-start(bf16[128,8,128]{2,0,1:T(8,128)(2,1)} %copy.90), calls=%async_computation.1 | async-start | bytes 524288 | tf_op jit(solution)/shard_map/all_to_all | solution.py:84
  14.6 88.6 %all-gather.5.cloned.1.call-start = ((), (), s32[]{:S(2)}) async-start(), calls=%async_computation.7 | async-start | bytes 8912896 | tf_op jit(solution)/shard_map/all_gather | solution.py:28
  33.9 35.4 %all-to-all-start.2 = ((bf16[128,8,256]{0,2,1:T(8,128)(2,1)}), bf16[128,8,256]{0,2,1:T(8,128)(2,1)S(1)}, u32[]{:S(2)}, u32[]{:S(2)}) async-start(bf16[128,8,256]{0,2,1:T(8,128)(2,1)} %bitcast.8), calls=%async_computation.2 | async-start | bytes 1048576 | tf_op jit(solution)/shard_map/all_to_all | solution.py:81
  37.4 136.7 %all-gather.7.cloned.1.call-start = ((), (), s32[]{:S(2)}) async-start(), calls=%async_computation.8 | async-start | bytes 1114112 | tf_op jit(solution)/shard_map/all_gather | solution.py:121
  38.2 193.0 %reduce-scatter.3.cloned.1.call-start = ((), (), s32[]{:S(2)}) async-start(), calls=%async_computation.9 | async-start | bytes 4718592 | tf_op jit(solution)/shard_map/reduce_scatter | solution.py:123
  105.1 3.5 copy-start
  106.8 1.9 copy-start.15
  111.2 1.1 copy-start.6
  111.2 1.1 copy-start.14
  115.9 1.2 copy-start.5
  115.9 1.2 copy-start.13
  121.7 1.3 copy-start.4
  121.7 1.3 copy-start.12
  128.8 1.4 copy-start.3
  128.8 1.4 copy-start.11
  158.9 2.3 copy-start.2
  158.9 2.3 copy-start.10
  174.1 4.6 copy-start.9
  178.6 5.9 %copy-start.16 = (bf16[2048]{0:T(1024)(128)(2,1)S(1)}, bf16[2048]{0:T(1024)(128)(2,1)}, u32[]{:S(2)}) copy-start(bf16[2048]{0:T(1024)(128)(2,1)} %param.14) | copy-start | bytes 12292
  178.6 52.6 %copy-start.8 = (bf16[128,2048]{1,0:T(8,128)(2,1)S(1)}, bf16[128,2048]{1,0:T(8,128)(2,1)}, u32[]{:S(2)}) copy-start(bf16[128,2048]{1,0:T(8,128)(2,1)} %param.9) | copy-start | bytes 1572868
  180.1 52.7 %all-to-all-start.4 = ((bf16[8,256,448]{1,2,0:T(8,128)(2,1)}), bf16[8,256,448]{1,2,0:T(8,128)(2,1)S(1)}, u32[]{:S(2)}, u32[]{:S(2)}) async-start(bf16[8,256,448]{1,2,0:T(8,128)(2,1)} %broadcast_in_dim.157), calls=%async_computation.5 | async-start | bytes 3670016 | tf_op jit(solution)/shard_map/all_to_all | solution.py:37
  232.5 272.6 %copy-start.1 = (bf16[128,2048]{1,0:T(8,128)(2,1)}, bf16[128,2048]{1,0:T(8,128)(2,1)S(1)}, u32[]{:S(2)}) copy-start(bf16[128,2048]{1,0:T(8,128)(2,1)S(1)} %get-tuple-element.3) | copy-start | bytes 1572868
  237.1 133.2 %all-to-all-start.3 = ((bf16[16,128,2048]{2,1,0:T(8,128)(2,1)}), bf16[16,128,2048]{2,1,0:T(8,128)(2,1)}, u32[]{:S(2)}, u32[]{:S(2)}) async-start(bf16[16,128,2048]{2,1,0:T(8,128)(2,1)} %stack.2), calls=%async_computation.4 | async-start | bytes 16777216 | tf_op jit(solution)/shard_map/all_to_all | solution.py:13
  243.7 136.2 %all-gather.9.cloned.1.call-start = ((), (), s32[]{:S(2)}) async-start(), calls=%async_computation.10 | async-start | bytes 2064384 | tf_op jit(solution)/shard_map/all_gather | solution.py:141
  244.3 144.8 %all-gather.11.cloned.1.call-start = ((), (), s32[]{:S(2)}) async-start(), calls=%async_computation.11 | async-start | bytes 2064384 | tf_op jit(solution)/shard_map/all_gather | solution.py:143
  244.9 260.3 %reduce-scatter.5.cloned.1.call-start = ((), (), s32[]{:S(2)}) async-start(), calls=%async_computation.12 | async-start | bytes 8912896 | tf_op jit(solution)/shard_map/reduce_scatter | solution.py:145
Sparse Core Ops, SparseCore 0:
  33.0 70.1 all-gather.4
  105.3 42.6 all-gather.6
  178.8 52.3 reduce-scatter.2
  245.9 25.1 all-gather.8
  272.7 26.8 all-gather.10
  397.5 107.6 reduce-scatter.4
